TPU v7x, 512 devices: a whole 4x8x8 slice. The times are simulated.
512 devices in a mesh: seq: 64 (over z_hi, x, y), head: 8 (over z_lo, core).
Axes of the slice: x: 4, y: 8, z: 8 (z_hi: 2, z_lo: 4; z = z_hi * 4 + z_lo), core: 2. Of those that a mesh axis runs over, the one named last changes fastest.
Arguments:
- queries: bfloat16 [12288, 32, 128], P('seq', 'head'), may hold values from -180 to 180
- key_rows: bfloat16 [12288, 8, 128], P('seq', 'head'), may hold values from -4.5 to 4.5
- value_rows: bfloat16 [12288, 8, 128], P('seq', 'head'), may hold values from -24 to 24
- windows: int32 [32], P('head'), may hold values from 768 to 1536, as said below
- sink_counts: int32 [32], P('head'), may hold values from 1 to 4, as said below
- sink_bias: float32 [32], P('head'), may hold values from 3 to 7
- out_weight: bfloat16 [4096, 4096], P('head'), may hold values from -0.09375 to 0.09375
Outputs:
- attn_out: bfloat16 [12288, 4096], P(('seq', 'head'))
Inputs may be any that keep to these rules, and one draw needn't show every extreme that they name: `windows`: each head's window lies between 768 and 1536, and some head has exactly 1536. `sink_counts`: each head has 1 to 4 sink tokens, and some head has exactly 4.
All inputs are finite; a program needn't handle non-finite values.
Results may differ from a plain program's by a relative error of at most 0.018.
Values may be sent and summed in bfloat16 or wider, within the bound.
A program may use at most 64 MiB of HBM per device.

v0:
```python
import jax
import jax.numpy as jnp
from jax import lax
from jax.sharding import Mesh
from jax.sharding import PartitionSpec as P

WINDOW = 1536
SINKS = 4
SEQ = ("seq_0", "seq_1", "seq_2")
SEQ_HEAD = ("seq_0", "seq_1", "seq_2", "head")


def shifted(block, axis, distance):
    devices = range(lax.axis_size(axis))
    route = [(i - distance, i) for i in devices if i - distance in devices]
    return lax.ppermute(block, axis, route)


def broadcast_by_axis(shard, axes, root):
    shard = jnp.where(lax.axis_index(axes) == root, shard, jnp.zeros_like(shard))
    for axis in axes:
        shard = lax.psum(shard, axis)
    return shard


def cut_along(shard, dim, length):
    dims = shard.shape
    blocks = shard.reshape(*dims[:dim], length, dims[dim] // length, *dims[dim + 1 :])
    return jnp.moveaxis(blocks, dim, 0)


def sent_and_summed(shard, axis, dim):
    blocks = cut_along(shard, dim, lax.axis_size(axis))
    arrived = lax.all_to_all(blocks, axis, split_axis=0, concat_axis=0, tiled=True)
    return arrived.astype(jnp.float32).sum(axis=0)


def attend_block(query_block, band_rows, sink_rows, first_pos, windows, sink_counts, sink_bias):
    tok_rows, local_heads, head_width = query_block.shape
    kv_local = band_rows.shape[2]
    group_size = local_heads // kv_local
    band_span = band_rows.shape[1]
    sink_total = sink_rows.shape[1]
    all_keys = jnp.concatenate([sink_rows[0], band_rows[0]], axis=0)
    all_values = jnp.concatenate([sink_rows[1], band_rows[1]], axis=0)
    grouped = query_block.reshape(tok_rows, kv_local, group_size, head_width)
    score_scale = 1.0 / head_width**0.5
    scores = (
        jnp.einsum("tkgd,skd->kgts", grouped, all_keys, preferred_element_type=jnp.float32)
        * score_scale
    )
    query_pos = first_pos + jnp.arange(tok_rows, dtype=jnp.int32)
    band_pos = first_pos + tok_rows - band_span + jnp.arange(band_span, dtype=jnp.int32)
    sink_pos = jnp.arange(sink_total, dtype=jnp.int32)
    key_pos = jnp.concatenate([sink_pos, band_pos])
    is_sink = jnp.concatenate([jnp.ones((sink_total,), bool), jnp.zeros((band_span,), bool)])
    head_window = windows.reshape(kv_local, group_size, 1, 1)
    head_sinks = sink_counts.reshape(kv_local, group_size, 1, 1)
    head_bias = sink_bias.reshape(kv_local, group_size, 1, 1)
    distance = query_pos[:, None] - key_pos[None, :]
    visible = (distance >= 0) & jnp.where(
        is_sink, key_pos < head_sinks, (distance < head_window) & (key_pos >= head_sinks)
    )
    scores = scores + jnp.where(is_sink, head_bias, 0.0)
    masked = jnp.where(visible, scores, -1e30)
    highest = jnp.max(masked, axis=-1, keepdims=True)
    weights = jnp.where(visible, jnp.exp(masked - highest), 0.0)
    normed = (weights / jnp.sum(weights, axis=-1, keepdims=True)).astype(jnp.bfloat16)
    mixed = jnp.einsum("kgts,skd->tkgd", normed, all_values, preferred_element_type=jnp.float32)
    return mixed.astype(jnp.bfloat16).reshape(tok_rows, local_heads * head_width)


def shards(queries, key_rows, value_rows, windows, sink_counts, sink_bias, out_weight):
    tok_rows = queries.shape[0]
    stacked = jnp.stack([key_rows, value_rows])
    halo_depth = (WINDOW - 1) // tok_rows + 1
    received = [shifted(stacked, SEQ, halo_depth - number) for number in range(halo_depth)]
    halo_rows = jnp.concatenate(received, axis=1)
    band_all = jnp.concatenate([halo_rows, stacked], axis=1)
    sink_rows = broadcast_by_axis(stacked[:, :SINKS], SEQ, 0)
    first_pos = lax.axis_index(SEQ) * tok_rows
    attended = attend_block(
        queries, band_all, sink_rows, first_pos, windows, sink_counts, sink_bias
    )
    mine = sent_and_summed(
        jnp.dot(attended, out_weight, preferred_element_type=jnp.float32).astype(jnp.bfloat16),
        "head",
        0,
    )
    return mine.astype(jnp.bfloat16)


def solution(mesh):
    split = Mesh(
        mesh.devices.reshape(2, 4, 8, mesh.shape["head"]), ("seq_0", "seq_1", "seq_2", "head")
    )
    return jax.shard_map(
        shards,
        mesh=split,
        in_specs=(
            P(SEQ, "head", None),
            P(SEQ, "head", None),
            P(SEQ, "head", None),
            P("head"),
            P("head"),
            P("head"),
            P("head", None),
        ),
        out_specs=P(SEQ_HEAD, None),
        check_vma=False,
    )
```

profile of v0, /device:TPU:256, one launch (start us, length us, event | category | flops | bytes accessed | tf_op | source)
XLA Modules:
  0.0 160.0 jit_solution(8025812477693680216)
XLA Ops:
  0.0 0.0 copy-start
  0.0 0.0 copy-start.2
  0.0 0.0 copy-start.3
  0.0 0.9 pad_maximum_fusion
  0.9 4.5 %collective-permute-start.6 = (bf16[2,192,1,128]{3,1,2,0:T(8,128)(2,1)S(1)}, bf16[2,192,1,128]{3,1,2,0:T(8,128)(2,1)S(1)}, u32[]{:S(2)}, u32[]{:S(2)}) collective-permute-start(bf16[2,192,1,128]{3,1,2,0:T(8,128)(2,1)S(1)} %pad_maximum_fusion), channel_id=1, source_target_pairs={{0,16},{8,24},{16,32},{24,40},{32,48},{40,56},{48,64},{56,72},{64,... | collective-permute-start | bytes 294920 | tf_op jit(solution)/shard_map/ppermute | solution.py:16
  5.4 5.8 %collective-permute-start.5 = (bf16[2,192,1,128]{3,1,2,0:T(8,128)(2,1)S(1)}, bf16[2,192,1,128]{3,1,2,0:T(8,128)(2,1)S(1)}, u32[]{:S(2)}, u32[]{:S(2)}) collective-permute-start(bf16[2,192,1,128]{3,1,2,0:T(8,128)(2,1)S(1)} %pad_maximum_fusion), channel_id=1, source_target_pairs={{0,24},{8,32},{16,40},{24,48},{32,56},{40,64},{48,72},{56,80},{64,... | collective-permute-start | bytes 294920 | tf_op jit(solution)/shard_map/ppermute | solution.py:16
  11.2 3.8 %collective-permute-start.4 = (bf16[2,192,1,128]{3,1,2,0:T(8,128)(2,1)S(1)}, bf16[2,192,1,128]{3,1,2,0:T(8,128)(2,1)S(1)}, u32[]{:S(2)}, u32[]{:S(2)}) collective-permute-start(bf16[2,192,1,128]{3,1,2,0:T(8,128)(2,1)S(1)} %pad_maximum_fusion), channel_id=1, source_target_pairs={{0,32},{8,40},{16,48},{24,56},{32,64},{40,72},{48,80},{56,88},{64,... | collective-permute-start | bytes 294920 | tf_op jit(solution)/shard_map/ppermute | solution.py:16
  15.1 6.0 %collective-permute-start.3 = (bf16[2,192,1,128]{3,1,2,0:T(8,128)(2,1)S(1)}, bf16[2,192,1,128]{3,1,2,0:T(8,128)(2,1)S(1)}, u32[]{:S(2)}, u32[]{:S(2)}) collective-permute-start(bf16[2,192,1,128]{3,1,2,0:T(8,128)(2,1)S(1)} %pad_maximum_fusion), channel_id=1, source_target_pairs={{0,40},{8,48},{16,56},{24,64},{32,72},{40,80},{48,88},{56,96},{64,... | collective-permute-start | bytes 294920 | tf_op jit(solution)/shard_map/ppermute | solution.py:16
  21.1 3.4 %collective-permute-start = (bf16[2,192,1,128]{3,1,2,0:T(8,128)(2,1)S(1)}, bf16[2,192,1,128]{3,1,2,0:T(8,128)(2,1)S(1)}, u32[]{:S(2)}, u32[]{:S(2)}) collective-permute-start(bf16[2,192,1,128]{3,1,2,0:T(8,128)(2,1)S(1)} %pad_maximum_fusion), channel_id=1, source_target_pairs={{0,64},{8,72},{16,80},{24,88},{32,96},{40,104},{48,112},{56,120},{... | collective-permute-start | bytes 294920 | tf_op jit(solution)/shard_map/ppermute | solution.py:16
  24.6 0.1 pad_add_fusion
  24.7 0.3 broadcast_compare_fusion
  25.0 0.2 broadcast_subtract_fusion
  25.1 0.7 fusion.20
  25.8 8.8 %psum.21 = bf16[2,4,1,128]{3,1,2,0:T(4,128)(2,1)S(1)} all-reduce(bf16[2,4,1,128]{3,1,2,0:T(4,128)(2,1)S(1)} %fusion.20), channel_id=1, replica_groups=mesh['seq_0'=2,'seq_1'=4,'seq_2'=8,'head'=8] {'seq_0'}, use_global_device_ids=true, to_apply=%region_0.1 | all-reduce | flops 1024 | bytes 4096 | tf_op jit(solution)/shard_map/psum | solution.py:22
  34.7 9.5 %psum.22 = bf16[2,4,1,128]{3,1,2,0:T(4,128)(2,1)S(1)} all-reduce(bf16[2,4,1,128]{3,1,2,0:T(4,128)(2,1)S(1)} %psum.21), channel_id=1, replica_groups=mesh['seq_0'=2,'seq_1'=4,'seq_2'=8,'head'=8] {'seq_1'}, use_global_device_ids=true, to_apply=%region_1.2 | all-reduce | flops 1024 | bytes 4096 | tf_op jit(solution)/shard_map/psum | solution.py:22
  44.1 16.7 %psum.23 = bf16[2,4,1,128]{3,1,2,0:T(4,128)(2,1)S(1)} all-reduce(bf16[2,4,1,128]{3,1,2,0:T(4,128)(2,1)S(1)} %psum.22), channel_id=1, replica_groups=mesh['seq_0'=2,'seq_1'=4,'seq_2'=8,'head'=8] {'seq_2'}, use_global_device_ids=true, to_apply=%region_2.3 | all-reduce | flops 1024 | bytes 4096 | tf_op jit(solution)/shard_map/psum | solution.py:22
  60.8 0.7 broadcast_compare_fusion.2
  61.6 0.8 broadcast_select_fusion
  62.4 0.0 collective-permute-done
  62.4 3.9 %collective-permute-start.1 = (bf16[2,192,1,128]{3,1,2,0:T(8,128)(2,1)S(1)}, bf16[2,192,1,128]{3,1,2,0:T(8,128)(2,1)S(1)}, u32[]{:S(2)}, u32[]{:S(2)}) collective-permute-start(bf16[2,192,1,128]{3,1,2,0:T(8,128)(2,1)S(1)} %pad_maximum_fusion), channel_id=1, source_target_pairs={{0,56},{8,64},{16,72},{24,80},{32,88},{40,96},{48,104},{56,112},{6... | collective-permute-start | bytes 294920 | tf_op jit(solution)/shard_map/ppermute | solution.py:16
  66.3 9.5 %collective-permute-done.1 = bf16[2,192,1,128]{3,1,2,0:T(8,128)(2,1)S(1)} collective-permute-done((bf16[2,192,1,128]{3,1,2,0:T(8,128)(2,1)S(1)}, bf16[2,192,1,128]{3,1,2,0:T(8,128)(2,1)S(1)}, u32[]{:S(2)}, u32[]{:S(2)}) %collective-permute-start.1) | collective-permute-done | bytes 98336 | tf_op jit(solution)/shard_map/ppermute | solution.py:16
  75.8 3.3 %collective-permute-start.2 = (bf16[2,192,1,128]{3,1,2,0:T(8,128)(2,1)S(1)}, bf16[2,192,1,128]{3,1,2,0:T(8,128)(2,1)S(1)}, u32[]{:S(2)}, u32[]{:S(2)}) collective-permute-start(bf16[2,192,1,128]{3,1,2,0:T(8,128)(2,1)S(1)} %pad_maximum_fusion), channel_id=1, source_target_pairs={{0,48},{8,56},{16,64},{24,72},{32,80},{40,88},{48,96},{56,104},{64... | collective-permute-start | bytes 294920 | tf_op jit(solution)/shard_map/ppermute | solution.py:16
  79.2 10.9 %collective-permute-done.2 = bf16[2,192,1,128]{3,1,2,0:T(8,128)(2,1)S(1)} collective-permute-done((bf16[2,192,1,128]{3,1,2,0:T(8,128)(2,1)S(1)}, bf16[2,192,1,128]{3,1,2,0:T(8,128)(2,1)S(1)}, u32[]{:S(2)}, u32[]{:S(2)}) %collective-permute-start.2) | collective-permute-done | bytes 98336 | tf_op jit(solution)/shard_map/ppermute | solution.py:16
  90.1 5.0 %collective-permute-start.7 = (bf16[2,192,1,128]{3,1,2,0:T(8,128)(2,1)S(1)}, bf16[2,192,1,128]{3,1,2,0:T(8,128)(2,1)S(1)}, u32[]{:S(2)}, u32[]{:S(2)}) collective-permute-start(bf16[2,192,1,128]{3,1,2,0:T(8,128)(2,1)S(1)} %pad_maximum_fusion), channel_id=1, source_target_pairs={{0,8},{8,16},{16,24},{24,32},{32,40},{40,48},{48,56},{56,64},{64,7... | collective-permute-start | bytes 294920 | tf_op jit(solution)/shard_map/ppermute | solution.py:16
  95.1 0.0 collective-permute-done.3
  95.1 0.0 collective-permute-done.4
  95.2 0.0 collective-permute-done.5
  95.2 0.0 collective-permute-done.6
  95.2 9.5 %collective-permute-done.7 = bf16[2,192,1,128]{3,1,2,0:T(8,128)(2,1)S(1)} collective-permute-done((bf16[2,192,1,128]{3,1,2,0:T(8,128)(2,1)S(1)}, bf16[2,192,1,128]{3,1,2,0:T(8,128)(2,1)S(1)}, u32[]{:S(2)}, u32[]{:S(2)}) %collective-permute-start.7) | collective-permute-done | bytes 98336 | tf_op jit(solution)/shard_map/ppermute | solution.py:16
  104.7 0.8 constant_dynamic-update-slice_fusion
  105.6 0.1 slice_bitcast_fusion.1
  105.6 0.0 copy-done
  105.7 0.0 copy-done.2
  105.7 0.0 copy-done.3
  105.7 2.3 %fusion.1 = (f32[4,192]{1,0:T(4,128)S(1)}, f32[1732,192,4]{0,1,2:T(8,128)S(1)}) fusion(f32[4,1732]{1,0:T(4,128)S(1)} %broadcast_select_fusion, s32[192,1732]{1,0:T(8,128)S(1)} %broadcast_subtract_fusion, s32[4]{0:T(128)S(1)} %copy-done.3, pred[4,1732]{1,0:T(4,128)(4,1)S(1)} %get-tuple-element.8, pred[4,1732]{1,0:T(4,128)(4,1)S(1)} %get-tuple-element.7, ...), kind=kOutput, calls=%fused_computation.6 | convolution fusion | flops 352052480 | bytes 7669812 | tf_op jit(solution)/shard_map/tkgd,skd->kgts/dot_general | solution.py:49
  108.0 3.5 %fusion.4 = f32[4,192]{1,0:T(4,128)S(1)} fusion(f32[4,192]{1,0:T(4,128)S(1)} %get-tuple-element.11, f32[4,1732]{1,0:T(4,128)S(1)} %broadcast_select_fusion, f32[1732,192,4]{0,1,2:T(8,128)S(1)} %get-tuple-element.12, pred[4,1732]{1,0:T(4,128)(4,1)S(1)} %get-tuple-element.8, s32[4]{0:T(128)S(1)} %copy-done.3, s32[192,1732]{1,0:T(8,128)S(1)} %broadcast_subtract_fusion, ...), kind=kLoop, calls=%fused_computation.9 | loop fusion | flops 13300992 | bytes 7032884 | tf_op jit(solution)/shard_map/reduce_sum | solution.py:68
  111.5 0.0 copy-start.1
  111.5 2.8 %fusion.8 = bf16[192,1,4,128]{3,0,2,1:T(8,128)(2,1)S(1)} fusion(f32[4,192]{1,0:T(4,128)S(1)} %fusion.4, f32[4,192]{1,0:T(4,128)S(1)} %get-tuple-element.11, f32[4,1732]{1,0:T(4,128)S(1)} %broadcast_select_fusion, f32[1732,192,4]{0,1,2:T(8,128)S(1)} %get-tuple-element.12, pred[4,1732]{1,0:T(4,128)(4,1)S(1)} %get-tuple-element.8, s32[4]{0:T(128)S(1)} %copy-done.3, ...), kind=kOutput, calls=%fused_computation.11 | convolution fusion | flops 356142080 | bytes 7672884 | tf_op jit(solution)/shard_map/kgts,skd->tkgd/dot_general | solution.py:69
  114.4 0.2 copy.10
  114.5 0.0 copy-done.1
  114.5 1.0 convolution_convert_fusion
  115.5 43.5 %all_to_all.5 = bf16[8,24,4096]{2,1,0:T(8,128)(2,1)S(1)} all-to-all(bf16[8,24,4096]{2,1,0:T(8,128)(2,1)S(1)} %bitcast.58), channel_id=1, replica_groups=mesh['seq_0'=2,'seq_1'=4,'seq_2'=8,'head'=8] {'head'}, dimensions={0} | all-to-all | bytes 3145728 | tf_op jit(solution)/shard_map/all_to_all | solution.py:34
  159.1 0.9 reduce_sum.22
  (12 shorter events, 0.1 us)
Async XLA Ops:
  0.0 105.7 %copy-start = (bf16[192,4,128]{2,1,0:T(4,128)(2,1)S(1)}, bf16[192,4,128]{2,1,0:T(4,128)(2,1)}, u32[]{:S(2)}) copy-start(bf16[192,4,128]{2,1,0:T(4,128)(2,1)} %param.7) | copy-start | bytes 589828
  0.0 105.7 %copy-start.2 = (pred[1732]{0:T(1024)(128)(4,1)S(1)}, pred[1732]{0:T(1024)(128)(4,1)}, u32[]{:S(2)}) copy-start(pred[1732]{0:T(1024)(128)(4,1)} %constant.37.clone.1) | copy-start | bytes 5200
  0.0 105.7 %copy-start.3 = (s32[4]{0:T(128)S(1)}, s32[4]{0:T(128)}, u32[]{:S(2)}) copy-start(s32[4]{0:T(128)} %param.10) | copy-start | bytes 52
  0.9 94.3 %collective-permute-start.6 = (bf16[2,192,1,128]{3,1,2,0:T(8,128)(2,1)S(1)}, bf16[2,192,1,128]{3,1,2,0:T(8,128)(2,1)S(1)}, u32[]{:S(2)}, u32[]{:S(2)}) collective-permute-start(bf16[2,192,1,128]{3,1,2,0:T(8,128)(2,1)S(1)} %pad_maximum_fusion), channel_id=1, source_target_pairs={{0,16},{8,24},{16,32},{24,40},{32,48},{40,56},{48,64},{56,72},{64,... | collective-permute-start | bytes 294920 | tf_op jit(solution)/shard_map/ppermute | solution.py:16
  5.4 89.8 %collective-permute-start.5 = (bf16[2,192,1,128]{3,1,2,0:T(8,128)(2,1)S(1)}, bf16[2,192,1,128]{3,1,2,0:T(8,128)(2,1)S(1)}, u32[]{:S(2)}, u32[]{:S(2)}) collective-permute-start(bf16[2,192,1,128]{3,1,2,0:T(8,128)(2,1)S(1)} %pad_maximum_fusion), channel_id=1, source_target_pairs={{0,24},{8,32},{16,40},{24,48},{32,56},{40,64},{48,72},{56,80},{64,... | collective-permute-start | bytes 294920 | tf_op jit(solution)/shard_map/ppermute | solution.py:16
  11.2 83.9 %collective-permute-start.4 = (bf16[2,192,1,128]{3,1,2,0:T(8,128)(2,1)S(1)}, bf16[2,192,1,128]{3,1,2,0:T(8,128)(2,1)S(1)}, u32[]{:S(2)}, u32[]{:S(2)}) collective-permute-start(bf16[2,192,1,128]{3,1,2,0:T(8,128)(2,1)S(1)} %pad_maximum_fusion), channel_id=1, source_target_pairs={{0,32},{8,40},{16,48},{24,56},{32,64},{40,72},{48,80},{56,88},{64,... | collective-permute-start | bytes 294920 | tf_op jit(solution)/shard_map/ppermute | solution.py:16
  15.1 80.0 %collective-permute-start.3 = (bf16[2,192,1,128]{3,1,2,0:T(8,128)(2,1)S(1)}, bf16[2,192,1,128]{3,1,2,0:T(8,128)(2,1)S(1)}, u32[]{:S(2)}, u32[]{:S(2)}) collective-permute-start(bf16[2,192,1,128]{3,1,2,0:T(8,128)(2,1)S(1)} %pad_maximum_fusion), channel_id=1, source_target_pairs={{0,40},{8,48},{16,56},{24,64},{32,72},{40,80},{48,88},{56,96},{64,... | collective-permute-start | bytes 294920 | tf_op jit(solution)/shard_map/ppermute | solution.py:16
  21.1 41.2 %collective-permute-start = (bf16[2,192,1,128]{3,1,2,0:T(8,128)(2,1)S(1)}, bf16[2,192,1,128]{3,1,2,0:T(8,128)(2,1)S(1)}, u32[]{:S(2)}, u32[]{:S(2)}) collective-permute-start(bf16[2,192,1,128]{3,1,2,0:T(8,128)(2,1)S(1)} %pad_maximum_fusion), channel_id=1, source_target_pairs={{0,64},{8,72},{16,80},{24,88},{32,96},{40,104},{48,112},{56,120},{... | collective-permute-start | bytes 294920 | tf_op jit(solution)/shard_map/ppermute | solution.py:16
  62.4 13.4 %collective-permute-start.1 = (bf16[2,192,1,128]{3,1,2,0:T(8,128)(2,1)S(1)}, bf16[2,192,1,128]{3,1,2,0:T(8,128)(2,1)S(1)}, u32[]{:S(2)}, u32[]{:S(2)}) collective-permute-start(bf16[2,192,1,128]{3,1,2,0:T(8,128)(2,1)S(1)} %pad_maximum_fusion), channel_id=1, source_target_pairs={{0,56},{8,64},{16,72},{24,80},{32,88},{40,96},{48,104},{56,112},{6... | collective-permute-start | bytes 294920 | tf_op jit(solution)/shard_map/ppermute | solution.py:16
  75.8 14.3 %collective-permute-start.2 = (bf16[2,192,1,128]{3,1,2,0:T(8,128)(2,1)S(1)}, bf16[2,192,1,128]{3,1,2,0:T(8,128)(2,1)S(1)}, u32[]{:S(2)}, u32[]{:S(2)}) collective-permute-start(bf16[2,192,1,128]{3,1,2,0:T(8,128)(2,1)S(1)} %pad_maximum_fusion), channel_id=1, source_target_pairs={{0,48},{8,56},{16,64},{24,72},{32,80},{40,88},{48,96},{56,104},{64... | collective-permute-start | bytes 294920 | tf_op jit(solution)/shard_map/ppermute | solution.py:16
  90.1 14.6 %collective-permute-start.7 = (bf16[2,192,1,128]{3,1,2,0:T(8,128)(2,1)S(1)}, bf16[2,192,1,128]{3,1,2,0:T(8,128)(2,1)S(1)}, u32[]{:S(2)}, u32[]{:S(2)}) collective-permute-start(bf16[2,192,1,128]{3,1,2,0:T(8,128)(2,1)S(1)} %pad_maximum_fusion), channel_id=1, source_target_pairs={{0,8},{8,16},{16,24},{24,32},{32,40},{40,48},{48,56},{56,64},{64,7... | collective-permute-start | bytes 294920 | tf_op jit(solution)/shard_map/ppermute | solution.py:16
  111.5 3.0 %copy-start.1 = (bf16[512,4096]{1,0:T(8,128)(2,1)S(1)}, bf16[512,4096]{1,0:T(8,128)(2,1)}, u32[]{:S(2)}) copy-start(bf16[512,4096]{1,0:T(8,128)(2,1)} %param.13) | copy-start | bytes 12582916
where the time goes:
time: 161 us; the launch traced here: 160 us
  blocking collectives  78.5 us (49%)
  starting transfers between devices  35.8 us (22%)
  waiting for transfers between devices  29.9 us (19%)
  other arithmetic  8.87 us (6%)
  matrix products  6.17 us (4%)
    all_to_all x1, blocking collectives, sent_and_summed(): lax.all_to_all(blocks, axis, split_axis=0, concat_axis=0, tiled=True)  43.5 us
    ppermute x8, starting transfers between devices, shifted(): return lax.ppermute(block, axis, route)  35.8 us
    psum x3, blocking collectives, broadcast_by_axis(): shard = lax.psum(shard, axis)  35 us
    ppermute x8, waiting for transfers between devices, shifted(): return lax.ppermute(block, axis, route)  29.9 us
    reduce_sum x1, other arithmetic, attend_block(): jnp.sum(weights, axis=-1, keepdims=True)  3.48 us
  transfers between devices with their start and end apart: 8, of which 3 were waited for; matrix products, arithmetic and copies ran while one was open for 2% of the time, Pallas kernels for 0%

commit v1 on v0

--- a/solution.py
+++ b/solution.py
@@ -19,7 +19,7 @@
 def broadcast_by_axis(shard, axes, root):
     shard = jnp.where(lax.axis_index(axes) == root, shard, jnp.zeros_like(shard))
     for axis in axes:
-        shard = lax.psum(shard, axis)
+        shard = jnp.sum(lax.all_gather(shard, axis), axis=0)
     return shard
 
 

time: 161 us -> 169 us (1.050)
  blocking collectives: 78.5 us -> 86.2 us
  waiting for transfers between devices: 29.9 us -> 35.8 us
  starting transfers between devices: 35.8 us -> 30.5 us
    all_gather x0 -> x3, blocking collectives: none -> 42.7 us  [broadcast_by_axis(): shard = jnp.sum(lax.all_gather(shard, axis), axis=0)]
    psum x3 -> x0, blocking collectives: 35 us -> none  [broadcast_by_axis(): shard = lax.psum(shard, axis)]
    ppermute x8, waiting for transfers between devices: 29.9 us -> 35.8 us  [shifted(): return lax.ppermute(block, axis, route)]
    ppermute x8, starting transfers between devices: 35.8 us -> 30.5 us  [shifted(): return lax.ppermute(block, axis, route)]
where the time goes in v1:
time: 169 us; the launch traced here: 168 us
  blocking collectives  86.2 us (51%)
  waiting for transfers between devices  35.8 us (21%)
  starting transfers between devices  30.5 us (18%)
  other arithmetic  8.92 us (5%)
  matrix products  6.18 us (4%)
    all_to_all x1, blocking collectives, sent_and_summed(): lax.all_to_all(blocks, axis, split_axis=0, concat_axis=0, tiled=True)  43.5 us
    all_gather x3, blocking collectives, broadcast_by_axis(): shard = jnp.sum(lax.all_gather(shard, axis), axis=0)  42.7 us
    ppermute x8, waiting for transfers between devices, shifted(): return lax.ppermute(block, axis, route)  35.8 us
    ppermute x8, starting transfers between devices, shifted(): return lax.ppermute(block, axis, route)  30.5 us
    reduce_sum x1, other arithmetic, attend_block(): jnp.sum(weights, axis=-1, keepdims=True)  3.48 us
  transfers between devices with their start and end apart: 8, of which 3 were waited for; matrix products, arithmetic and copies ran while one was open for 2% of the time, Pallas kernels for 0%

profile of v1, /device:TPU:256, one launch (start us, length us, event | category | flops | bytes accessed | tf_op | source)
XLA Modules:
  0.0 168.2 jit_solution(15527921884242209961)
XLA Ops:
  0.0 0.0 copy-start
  0.0 0.0 copy-start.2
  0.0 0.0 copy-start.3
  0.0 0.9 pad_maximum_fusion
  0.9 4.5 %collective-permute-start.6 = (bf16[2,192,1,128]{3,1,2,0:T(8,128)(2,1)S(1)}, bf16[2,192,1,128]{3,1,2,0:T(8,128)(2,1)S(1)}, u32[]{:S(2)}, u32[]{:S(2)}) collective-permute-start(bf16[2,192,1,128]{3,1,2,0:T(8,128)(2,1)S(1)} %pad_maximum_fusion), channel_id=1, source_target_pairs={{0,16},{8,24},{16,32},{24,40},{32,48},{40,56},{48,64},{56,72},{64,... | collective-permute-start | bytes 294920 | tf_op jit(solution)/shard_map/ppermute | solution.py:16
  5.4 5.8 %collective-permute-start.5 = (bf16[2,192,1,128]{3,1,2,0:T(8,128)(2,1)S(1)}, bf16[2,192,1,128]{3,1,2,0:T(8,128)(2,1)S(1)}, u32[]{:S(2)}, u32[]{:S(2)}) collective-permute-start(bf16[2,192,1,128]{3,1,2,0:T(8,128)(2,1)S(1)} %pad_maximum_fusion), channel_id=1, source_target_pairs={{0,24},{8,32},{16,40},{24,48},{32,56},{40,64},{48,72},{56,80},{64,... | collective-permute-start | bytes 294920 | tf_op jit(solution)/shard_map/ppermute | solution.py:16
  11.2 3.8 %collective-permute-start.4 = (bf16[2,192,1,128]{3,1,2,0:T(8,128)(2,1)S(1)}, bf16[2,192,1,128]{3,1,2,0:T(8,128)(2,1)S(1)}, u32[]{:S(2)}, u32[]{:S(2)}) collective-permute-start(bf16[2,192,1,128]{3,1,2,0:T(8,128)(2,1)S(1)} %pad_maximum_fusion), channel_id=1, source_target_pairs={{0,32},{8,40},{16,48},{24,56},{32,64},{40,72},{48,80},{56,88},{64,... | collective-permute-start | bytes 294920 | tf_op jit(solution)/shard_map/ppermute | solution.py:16
  15.1 6.0 %collective-permute-start.3 = (bf16[2,192,1,128]{3,1,2,0:T(8,128)(2,1)S(1)}, bf16[2,192,1,128]{3,1,2,0:T(8,128)(2,1)S(1)}, u32[]{:S(2)}, u32[]{:S(2)}) collective-permute-start(bf16[2,192,1,128]{3,1,2,0:T(8,128)(2,1)S(1)} %pad_maximum_fusion), channel_id=1, source_target_pairs={{0,40},{8,48},{16,56},{24,64},{32,72},{40,80},{48,88},{56,96},{64,... | collective-permute-start | bytes 294920 | tf_op jit(solution)/shard_map/ppermute | solution.py:16
  21.1 3.4 %collective-permute-start = (bf16[2,192,1,128]{3,1,2,0:T(8,128)(2,1)S(1)}, bf16[2,192,1,128]{3,1,2,0:T(8,128)(2,1)S(1)}, u32[]{:S(2)}, u32[]{:S(2)}) collective-permute-start(bf16[2,192,1,128]{3,1,2,0:T(8,128)(2,1)S(1)} %pad_maximum_fusion), channel_id=1, source_target_pairs={{0,64},{8,72},{16,80},{24,88},{32,96},{40,104},{48,112},{56,120},{... | collective-permute-start | bytes 294920 | tf_op jit(solution)/shard_map/ppermute | solution.py:16
  24.6 0.1 pad_add_fusion
  24.7 0.3 broadcast_compare_fusion
  25.0 0.2 broadcast_subtract_fusion
  25.1 0.7 fusion.20
  25.8 8.3 %all-gather = bf16[4,4,1,128]{3,1,2,0:T(4,128)(2,1)S(1)} all-gather(bf16[2,4,1,128]{3,1,2,0:T(4,128)(2,1)S(1)} %fusion.20), channel_id=2, replica_groups=mesh['seq_0'=2,'seq_1'=4,'seq_2'=8,'head'=8] {'seq_0'}, dimensions={0}, use_global_device_ids=true | all-gather | bytes 6144 | tf_op jit(solution)/shard_map/all_gather | solution.py:22
  34.1 10.4 %all-gather.1 = bf16[8,4,128]{2,1,0:T(4,128)(2,1)S(1)} all-gather(bf16[2,4,128]{2,1,0:T(4,128)(2,1)S(1)} %reduce.9), channel_id=3, replica_groups=mesh['seq_0'=2,'seq_1'=4,'seq_2'=8,'head'=8] {'seq_1'}, dimensions={0}, use_global_device_ids=true | all-gather | bytes 10240 | tf_op jit(solution)/shard_map/all_gather | solution.py:22
  44.6 24.0 %all-gather.2 = bf16[16,4,128]{2,1,0:T(4,128)(2,1)S(1)} all-gather(bf16[2,4,128]{2,1,0:T(4,128)(2,1)S(1)} %reduce.10), channel_id=4, replica_groups=mesh['seq_0'=2,'seq_1'=4,'seq_2'=8,'head'=8] {'seq_2'}, dimensions={0}, use_global_device_ids=true | all-gather | bytes 18432 | tf_op jit(solution)/shard_map/all_gather | solution.py:22
  68.5 0.7 broadcast_compare_fusion.2
  69.3 0.8 broadcast_select_fusion
  70.1 0.0 collective-permute-done
  70.1 1.9 %collective-permute-start.1 = (bf16[2,192,1,128]{3,1,2,0:T(8,128)(2,1)S(1)}, bf16[2,192,1,128]{3,1,2,0:T(8,128)(2,1)S(1)}, u32[]{:S(2)}, u32[]{:S(2)}) collective-permute-start(bf16[2,192,1,128]{3,1,2,0:T(8,128)(2,1)S(1)} %pad_maximum_fusion), channel_id=1, source_target_pairs={{0,56},{8,64},{16,72},{24,80},{32,88},{40,96},{48,104},{56,112},{6... | collective-permute-start | bytes 294920 | tf_op jit(solution)/shard_map/ppermute | solution.py:16
  72.0 11.5 %collective-permute-done.1 = bf16[2,192,1,128]{3,1,2,0:T(8,128)(2,1)S(1)} collective-permute-done((bf16[2,192,1,128]{3,1,2,0:T(8,128)(2,1)S(1)}, bf16[2,192,1,128]{3,1,2,0:T(8,128)(2,1)S(1)}, u32[]{:S(2)}, u32[]{:S(2)}) %collective-permute-start.1) | collective-permute-done | bytes 98336 | tf_op jit(solution)/shard_map/ppermute | solution.py:16
  83.5 3.1 %collective-permute-start.2 = (bf16[2,192,1,128]{3,1,2,0:T(8,128)(2,1)S(1)}, bf16[2,192,1,128]{3,1,2,0:T(8,128)(2,1)S(1)}, u32[]{:S(2)}, u32[]{:S(2)}) collective-permute-start(bf16[2,192,1,128]{3,1,2,0:T(8,128)(2,1)S(1)} %pad_maximum_fusion), channel_id=1, source_target_pairs={{0,48},{8,56},{16,64},{24,72},{32,80},{40,88},{48,96},{56,104},{64... | collective-permute-start | bytes 294920 | tf_op jit(solution)/shard_map/ppermute | solution.py:16
  86.6 11.7 %collective-permute-done.2 = bf16[2,192,1,128]{3,1,2,0:T(8,128)(2,1)S(1)} collective-permute-done((bf16[2,192,1,128]{3,1,2,0:T(8,128)(2,1)S(1)}, bf16[2,192,1,128]{3,1,2,0:T(8,128)(2,1)S(1)}, u32[]{:S(2)}, u32[]{:S(2)}) %collective-permute-start.2) | collective-permute-done | bytes 98336 | tf_op jit(solution)/shard_map/ppermute | solution.py:16
  98.3 1.9 %collective-permute-start.7 = (bf16[2,192,1,128]{3,1,2,0:T(8,128)(2,1)S(1)}, bf16[2,192,1,128]{3,1,2,0:T(8,128)(2,1)S(1)}, u32[]{:S(2)}, u32[]{:S(2)}) collective-permute-start(bf16[2,192,1,128]{3,1,2,0:T(8,128)(2,1)S(1)} %pad_maximum_fusion), channel_id=1, source_target_pairs={{0,8},{8,16},{16,24},{24,32},{32,40},{40,48},{48,56},{56,64},{64,7... | collective-permute-start | bytes 294920 | tf_op jit(solution)/shard_map/ppermute | solution.py:16
  100.3 0.0 collective-permute-done.3
  100.3 0.0 collective-permute-done.4
  100.3 0.0 collective-permute-done.5
  100.4 0.0 collective-permute-done.6
  100.4 12.6 %collective-permute-done.7 = bf16[2,192,1,128]{3,1,2,0:T(8,128)(2,1)S(1)} collective-permute-done((bf16[2,192,1,128]{3,1,2,0:T(8,128)(2,1)S(1)}, bf16[2,192,1,128]{3,1,2,0:T(8,128)(2,1)S(1)}, u32[]{:S(2)}, u32[]{:S(2)}) %collective-permute-start.7) | collective-permute-done | bytes 98336 | tf_op jit(solution)/shard_map/ppermute | solution.py:16
  113.0 0.8 constant_dynamic-update-slice_fusion
  113.8 0.1 slice_bitcast_fusion.1
  113.9 0.0 copy-done
  113.9 0.0 copy-done.2
  113.9 0.0 copy-done.3
  113.9 2.3 %fusion.1 = (f32[4,192]{1,0:T(4,128)S(1)}, f32[1732,192,4]{0,1,2:T(8,128)S(1)}) fusion(f32[4,1732]{1,0:T(4,128)S(1)} %broadcast_select_fusion, s32[192,1732]{1,0:T(8,128)S(1)} %broadcast_subtract_fusion, s32[4]{0:T(128)S(1)} %copy-done.3, pred[4,1732]{1,0:T(4,128)(4,1)S(1)} %get-tuple-element.8, pred[4,1732]{1,0:T(4,128)(4,1)S(1)} %get-tuple-element.7, ...), kind=kOutput, calls=%fused_computation.6 | convolution fusion | flops 352052480 | bytes 7669812 | tf_op jit(solution)/shard_map/tkgd,skd->kgts/dot_general | solution.py:49
  116.2 3.5 %fusion.4 = f32[4,192]{1,0:T(4,128)S(1)} fusion(f32[4,192]{1,0:T(4,128)S(1)} %get-tuple-element.11, f32[4,1732]{1,0:T(4,128)S(1)} %broadcast_select_fusion, f32[1732,192,4]{0,1,2:T(8,128)S(1)} %get-tuple-element.12, pred[4,1732]{1,0:T(4,128)(4,1)S(1)} %get-tuple-element.8, s32[4]{0:T(128)S(1)} %copy-done.3, s32[192,1732]{1,0:T(8,128)S(1)} %broadcast_subtract_fusion, ...), kind=kLoop, calls=%fused_computation.9 | loop fusion | flops 13300992 | bytes 7032884 | tf_op jit(solution)/shard_map/reduce_sum | solution.py:68
  119.7 0.0 copy-start.1
  119.7 2.8 %fusion.8 = bf16[192,1,4,128]{3,0,2,1:T(8,128)(2,1)S(1)} fusion(f32[4,192]{1,0:T(4,128)S(1)} %fusion.4, f32[4,192]{1,0:T(4,128)S(1)} %get-tuple-element.11, f32[4,1732]{1,0:T(4,128)S(1)} %broadcast_select_fusion, f32[1732,192,4]{0,1,2:T(8,128)S(1)} %get-tuple-element.12, pred[4,1732]{1,0:T(4,128)(4,1)S(1)} %get-tuple-element.8, s32[4]{0:T(128)S(1)} %copy-done.3, ...), kind=kOutput, calls=%fused_computation.11 | convolution fusion | flops 356142080 | bytes 7672884 | tf_op jit(solution)/shard_map/kgts,skd->tkgd/dot_general | solution.py:69
  122.6 0.2 copy.12
  122.7 0.0 copy-done.1
  122.7 1.0 convolution_convert_fusion
  123.8 43.5 %all_to_all.5 = bf16[8,24,4096]{2,1,0:T(8,128)(2,1)S(1)} all-to-all(bf16[8,24,4096]{2,1,0:T(8,128)(2,1)S(1)} %bitcast.61), channel_id=1, replica_groups=mesh['seq_0'=2,'seq_1'=4,'seq_2'=8,'head'=8] {'head'}, dimensions={0} | all-to-all | bytes 3145728 | tf_op jit(solution)/shard_map/all_to_all | solution.py:34
  167.3 0.9 reduce_sum.61
  (15 shorter events, 0.2 us)
Async XLA Ops:
  0.0 113.9 %copy-start = (bf16[192,4,128]{2,1,0:T(4,128)(2,1)S(1)}, bf16[192,4,128]{2,1,0:T(4,128)(2,1)}, u32[]{:S(2)}) copy-start(bf16[192,4,128]{2,1,0:T(4,128)(2,1)} %param.7) | copy-start | bytes 589828
  0.0 113.9 %copy-start.2 = (pred[1732]{0:T(1024)(128)(4,1)S(1)}, pred[1732]{0:T(1024)(128)(4,1)}, u32[]{:S(2)}) copy-start(pred[1732]{0:T(1024)(128)(4,1)} %constant.40.clone.1) | copy-start | bytes 5200
  0.0 113.9 %copy-start.3 = (s32[4]{0:T(128)S(1)}, s32[4]{0:T(128)}, u32[]{:S(2)}) copy-start(s32[4]{0:T(128)} %param.10) | copy-start | bytes 52
  0.9 99.5 %collective-permute-start.6 = (bf16[2,192,1,128]{3,1,2,0:T(8,128)(2,1)S(1)}, bf16[2,192,1,128]{3,1,2,0:T(8,128)(2,1)S(1)}, u32[]{:S(2)}, u32[]{:S(2)}) collective-permute-start(bf16[2,192,1,128]{3,1,2,0:T(8,128)(2,1)S(1)} %pad_maximum_fusion), channel_id=1, source_target_pairs={{0,16},{8,24},{16,32},{24,40},{32,48},{40,56},{48,64},{56,72},{64,... | collective-permute-start | bytes 294920 | tf_op jit(solution)/shard_map/ppermute | solution.py:16
  5.4 94.9 %collective-permute-start.5 = (bf16[2,192,1,128]{3,1,2,0:T(8,128)(2,1)S(1)}, bf16[2,192,1,128]{3,1,2,0:T(8,128)(2,1)S(1)}, u32[]{:S(2)}, u32[]{:S(2)}) collective-permute-start(bf16[2,192,1,128]{3,1,2,0:T(8,128)(2,1)S(1)} %pad_maximum_fusion), channel_id=1, source_target_pairs={{0,24},{8,32},{16,40},{24,48},{32,56},{40,64},{48,72},{56,80},{64,... | collective-permute-start | bytes 294920 | tf_op jit(solution)/shard_map/ppermute | solution.py:16
  11.2 89.1 %collective-permute-start.4 = (bf16[2,192,1,128]{3,1,2,0:T(8,128)(2,1)S(1)}, bf16[2,192,1,128]{3,1,2,0:T(8,128)(2,1)S(1)}, u32[]{:S(2)}, u32[]{:S(2)}) collective-permute-start(bf16[2,192,1,128]{3,1,2,0:T(8,128)(2,1)S(1)} %pad_maximum_fusion), channel_id=1, source_target_pairs={{0,32},{8,40},{16,48},{24,56},{32,64},{40,72},{48,80},{56,88},{64,... | collective-permute-start | bytes 294920 | tf_op jit(solution)/shard_map/ppermute | solution.py:16
  15.1 85.2 %collective-permute-start.3 = (bf16[2,192,1,128]{3,1,2,0:T(8,128)(2,1)S(1)}, bf16[2,192,1,128]{3,1,2,0:T(8,128)(2,1)S(1)}, u32[]{:S(2)}, u32[]{:S(2)}) collective-permute-start(bf16[2,192,1,128]{3,1,2,0:T(8,128)(2,1)S(1)} %pad_maximum_fusion), channel_id=1, source_target_pairs={{0,40},{8,48},{16,56},{24,64},{32,72},{40,80},{48,88},{56,96},{64,... | collective-permute-start | bytes 294920 | tf_op jit(solution)/shard_map/ppermute | solution.py:16
  21.1 48.9 %collective-permute-start = (bf16[2,192,1,128]{3,1,2,0:T(8,128)(2,1)S(1)}, bf16[2,192,1,128]{3,1,2,0:T(8,128)(2,1)S(1)}, u32[]{:S(2)}, u32[]{:S(2)}) collective-permute-start(bf16[2,192,1,128]{3,1,2,0:T(8,128)(2,1)S(1)} %pad_maximum_fusion), channel_id=1, source_target_pairs={{0,64},{8,72},{16,80},{24,88},{32,96},{40,104},{48,112},{56,120},{... | collective-permute-start | bytes 294920 | tf_op jit(solution)/shard_map/ppermute | solution.py:16
  70.1 13.4 %collective-permute-start.1 = (bf16[2,192,1,128]{3,1,2,0:T(8,128)(2,1)S(1)}, bf16[2,192,1,128]{3,1,2,0:T(8,128)(2,1)S(1)}, u32[]{:S(2)}, u32[]{:S(2)}) collective-permute-start(bf16[2,192,1,128]{3,1,2,0:T(8,128)(2,1)S(1)} %pad_maximum_fusion), channel_id=1, source_target_pairs={{0,56},{8,64},{16,72},{24,80},{32,88},{40,96},{48,104},{56,112},{6... | collective-permute-start | bytes 294920 | tf_op jit(solution)/shard_map/ppermute | solution.py:16
  83.5 14.8 %collective-permute-start.2 = (bf16[2,192,1,128]{3,1,2,0:T(8,128)(2,1)S(1)}, bf16[2,192,1,128]{3,1,2,0:T(8,128)(2,1)S(1)}, u32[]{:S(2)}, u32[]{:S(2)}) collective-permute-start(bf16[2,192,1,128]{3,1,2,0:T(8,128)(2,1)S(1)} %pad_maximum_fusion), channel_id=1, source_target_pairs={{0,48},{8,56},{16,64},{24,72},{32,80},{40,88},{48,96},{56,104},{64... | collective-permute-start | bytes 294920 | tf_op jit(solution)/shard_map/ppermute | solution.py:16
  98.3 14.6 %collective-permute-start.7 = (bf16[2,192,1,128]{3,1,2,0:T(8,128)(2,1)S(1)}, bf16[2,192,1,128]{3,1,2,0:T(8,128)(2,1)S(1)}, u32[]{:S(2)}, u32[]{:S(2)}) collective-permute-start(bf16[2,192,1,128]{3,1,2,0:T(8,128)(2,1)S(1)} %pad_maximum_fusion), channel_id=1, source_target_pairs={{0,8},{8,16},{16,24},{24,32},{32,40},{40,48},{48,56},{56,64},{64,7... | collective-permute-start | bytes 294920 | tf_op jit(solution)/shard_map/ppermute | solution.py:16
  119.7 3.0 %copy-start.1 = (bf16[512,4096]{1,0:T(8,128)(2,1)S(1)}, bf16[512,4096]{1,0:T(8,128)(2,1)}, u32[]{:S(2)}) copy-start(bf16[512,4096]{1,0:T(8,128)(2,1)} %param.13) | copy-start | bytes 12582916
